TPU v7x, 32 devices: a whole 2x2x4 slice. The times are simulated.
32 devices in a mesh: expert: 4 (over z), tensor: 8 (over y, x, core).
Axes of the slice: x: 2, y: 2, z: 4, core: 2. Of those that a mesh axis runs over, the one named last changes fastest.
Arguments:
- layer_input: bfloat16 [8192, 2048], P('expert'), may hold values from -6 to 6
- cotangent: bfloat16 [8192, 2048], P(('expert', 'tensor')), may hold values from -6 to 6
- lengths: int32 [4, 4], P('expert'), may hold values from 1 to 1024, 2048 in all within a row
- routes: int32 [8192, 8], P(('expert', 'tensor')), may hold values from 0 to 15, all different within a row; in each aligned block of 256 rows (0 to 255, 256 to 511, ...) at most 192 rows name the same one
- attn_gain: float32 [2048], replicated, may hold values from 0.5 to 1.5
- w_qkv: bfloat16 [2048, 3, 2048], P(None, None, 'tensor'), may hold values from -0.125 to 0.125
- q_gain: float32 [128], replicated, may hold values from 0.6 to 5
- k_gain: float32 [128], replicated, may hold values from 0.6 to 5
- w_out: bfloat16 [2048, 2048], P('tensor'), may hold values from -2 to 2
- ffn_gain: float32 [2048], replicated, may hold values from 0.5 to 1.5
- w_router: bfloat16 [2048, 16], replicated, may hold values from -0.125 to 0.125
- w_gate: bfloat16 [16, 2048, 1024], P('expert', None, 'tensor'), may hold values from -0.125 to 0.125
- w_up: bfloat16 [16, 2048, 1024], P('expert', None, 'tensor'), may hold values from -0.125 to 0.125
- w_down: bfloat16 [16, 1024, 2048], P('expert', 'tensor'), may hold values from -6 to 6
Outputs:
- output: bfloat16 [8192, 2048], P(('expert', 'tensor'))
- grad_input: bfloat16 [8192, 2048], P(('expert', 'tensor'))
- grad_attn_gain: float32 [2048], replicated
- grad_w_qkv: float32 [2048, 3, 2048], P(None, None, 'tensor')
- grad_q_gain: float32 [128], replicated
- grad_k_gain: float32 [128], replicated
- grad_w_out: float32 [2048, 2048], P('tensor')
- grad_ffn_gain: float32 [2048], replicated
- grad_w_router: float32 [2048, 16], replicated
- grad_w_gate: float32 [16, 2048, 1024], P('expert', None, 'tensor')
- grad_w_up: float32 [16, 2048, 1024], P('expert', None, 'tensor')
- grad_w_down: float32 [16, 1024, 2048], P('expert', 'tensor')
Inputs may be any that keep to these rules, and one draw needn't show every extreme that they name: `routes`: no expert is named by more than 192 of the 256 rows of one device (aligned blocks of rows); in every draw some expert is named 192 times in some block. `lengths`: each row sums to 2048; its longest sequence has exactly 1024 tokens.
All inputs are finite; a program needn't handle non-finite values.
Results may differ from a plain program's by a relative error of at most 0.024.
The roundings to bfloat16 on the way count: a program that leaves them out, or rounds other values in their place, can miss the bound.
Values may be sent and summed in bfloat16 or wider, within the bound.
A program may use at most 384 MiB of HBM per device.

v0:
```python
import math
import jax
import jax.numpy as jnp
from jax import lax
from jax.sharding import PartitionSpec as P

NORM_EPS = 1e-06
ROPE_BASE = 50000.0


def rms_scale(values):
    return lax.rsqrt(jnp.mean(values * values, axis=-1, keepdims=True) + NORM_EPS)


def positions_of(seq_lengths, row_count):
    seq_ends = jnp.cumsum(seq_lengths)
    starts = seq_ends - seq_lengths
    row_index = jnp.arange(row_count, dtype=jnp.int32)
    segment = jnp.sum((row_index[:, None] >= seq_ends[None, :]).astype(jnp.int32), axis=1)
    picked = segment[:, None] == jnp.arange(seq_lengths.shape[0], dtype=jnp.int32)[None, :]
    offsets = jnp.sum(jnp.where(picked, starts[None, :], 0), axis=1)
    return (segment, row_index - offsets)


def rotate(values, position):
    half_width = values.shape[-1] // 2
    frequency = jnp.exp(
        jnp.arange(half_width, dtype=jnp.float32) * (-2.0 * math.log(ROPE_BASE) / values.shape[-1])
    )
    angle = position.astype(jnp.float32)[:, None] * frequency[None, :]
    cosine = jnp.cos(angle)[:, None, :]
    sine_part = jnp.sin(angle)[:, None, :]
    first_half = values[..., :half_width]
    second = values[..., half_width:]
    return jnp.concatenate(
        [first_half * cosine - second * sine_part, second * cosine + first_half * sine_part],
        axis=-1,
    )


def shape_heads(qkv_proj, q_gain, k_gain, position):
    query_rows = qkv_proj[:, 0]
    key_rows = qkv_proj[:, 1]
    value_rows = qkv_proj[:, 2]
    query_rows = rotate(query_rows * rms_scale(query_rows) * q_gain, position)
    key_rows = rotate(key_rows * rms_scale(key_rows) * k_gain, position)
    return (query_rows, key_rows, value_rows)


def masked_scores(query_block, key_rows, segment_block, segment, score_scale):
    scores = (
        jnp.einsum("qhd,khd->hqk", query_block, key_rows, preferred_element_type=jnp.float32)
        * score_scale
    )
    same_seq = (segment_block[:, None] == segment[None, :])[None]
    return jnp.where(same_seq, scores, -1e30)


def attend_forward(query_rows, key_rows, value_rows, segment, block_rows, score_scale):
    row_count, head_count, head_width = query_rows.shape
    block_count = row_count // block_rows

    def one_block(block_item):
        query_block, segment_block = block_item
        scores = masked_scores(query_block, key_rows, segment_block, segment, score_scale)
        row_peak = jnp.max(scores, axis=-1, keepdims=True)
        weights = jnp.exp(scores - row_peak)
        row_total = jnp.sum(weights, axis=-1, keepdims=True)
        probabilities = (weights / row_total).astype(jnp.bfloat16)
        mixed_out = jnp.einsum(
            "hqk,khd->qhd", probabilities, value_rows, preferred_element_type=jnp.float32
        )
        return (mixed_out, (row_peak + jnp.log(row_total))[..., 0])

    blocks = (
        query_rows.reshape(block_count, block_rows, head_count, head_width),
        segment.reshape(block_count, block_rows),
    )
    mixed_out, log_total = lax.map(one_block, blocks)
    return (mixed_out.reshape(row_count, head_count, head_width), log_total)


def attend_backward(
    query_rows, key_rows, value_rows, segment, grad_mixed, log_total, block_rows, score_scale
):
    row_count, head_count, head_width = query_rows.shape
    block_count = row_count // block_rows

    def one_block(carry, block_item):
        grad_keys, grad_values = carry
        query_block, segment_block, grad_block, total_block = block_item
        scores = masked_scores(query_block, key_rows, segment_block, segment, score_scale)
        probabilities = jnp.exp(scores - total_block[..., None])
        grad_probs = jnp.einsum(
            "qhd,khd->hqk", grad_block, value_rows, preferred_element_type=jnp.float32
        )
        delta = jnp.sum(grad_probs * probabilities, axis=-1, keepdims=True)
        grad_scores = (probabilities * (grad_probs - delta)).astype(jnp.bfloat16)
        grad_query = (
            jnp.einsum("hqk,khd->qhd", grad_scores, key_rows, preferred_element_type=jnp.float32)
            * score_scale
        )
        grad_keys = (
            grad_keys
            + jnp.einsum(
                "hqk,qhd->khd", grad_scores, query_block, preferred_element_type=jnp.float32
            )
            * score_scale
        )
        grad_values = grad_values + jnp.einsum(
            "hqk,qhd->khd",
            probabilities.astype(jnp.bfloat16),
            grad_block,
            preferred_element_type=jnp.float32,
        )
        return ((grad_keys, grad_values), grad_query)

    blocks = (
        query_rows.reshape(block_count, block_rows, head_count, head_width),
        segment.reshape(block_count, block_rows),
        grad_mixed.reshape(block_count, block_rows, head_count, head_width),
        log_total,
    )
    start_carry = (jnp.zeros(key_rows.shape, jnp.float32), jnp.zeros(value_rows.shape, jnp.float32))
    (grad_keys, grad_values), grad_query = lax.scan(one_block, start_carry, blocks)
    return (grad_query.reshape(row_count, head_count, head_width), grad_keys, grad_values)


def swiglu_back(grad_hidden, gate_pre, up_pre):
    sigmoid = jax.nn.sigmoid(gate_pre)
    grad_gate = grad_hidden * up_pre * sigmoid * (1.0 + gate_pre * (1.0 - sigmoid))
    grad_up = grad_hidden * gate_pre * sigmoid
    return (grad_gate.astype(jnp.bfloat16), grad_up.astype(jnp.bfloat16))


def body(
    layer_input,
    cotangent,
    lengths,
    routes,
    attn_gain,
    w_qkv,
    q_gain,
    k_gain,
    w_out,
    ffn_gain,
    w_router,
    w_gate,
    w_up,
    w_down,
):
    group_rows, model_width = layer_input.shape
    own_rows, top_count = routes.shape
    head_width = q_gain.shape[0]
    local_heads = w_qkv.shape[2] // head_width
    experts_all = w_router.shape[1]
    experts_here = w_gate.shape[0]
    senders = lax.axis_size("expert")
    tensor_rank = lax.axis_index("tensor")
    capacity = max(2, 3 * own_rows * top_count // (2 * experts_all))
    block_rows = min(512, group_rows)
    score_scale = 1.0 / math.sqrt(head_width)
    input_full = layer_input.astype(jnp.float32)
    scale_one = rms_scale(input_full)
    normed = (input_full * scale_one * attn_gain).astype(jnp.bfloat16)
    qkv_weight = w_qkv.reshape(model_width, 3 * local_heads * head_width)
    qkv_proj = jnp.dot(normed, qkv_weight, preferred_element_type=jnp.float32).reshape(
        group_rows, 3, local_heads, head_width
    )
    segment, position = positions_of(lengths[0], group_rows)

    def head_shapes(raw_proj, gain_q, gain_k):
        return shape_heads(raw_proj, gain_q, gain_k, position)

    (query_full, key_full, value_full), head_back = jax.vjp(head_shapes, qkv_proj, q_gain, k_gain)
    query_low = query_full.astype(jnp.bfloat16)
    key_low = key_full.astype(jnp.bfloat16)
    value_low = value_full.astype(jnp.bfloat16)
    mixed_full, log_total = attend_forward(
        query_low, key_low, value_low, segment, block_rows, score_scale
    )
    mixed_low = mixed_full.astype(jnp.bfloat16).reshape(group_rows, local_heads * head_width)
    row_part = mixed_low
    attn_own = lax.psum_scatter(
        jnp.dot(row_part, w_out, preferred_element_type=jnp.float32),
        "tensor",
        scatter_dimension=0,
        tiled=True,
    )
    input_own = lax.dynamic_slice_in_dim(input_full, tensor_rank * own_rows, own_rows, 0)
    scale_own = lax.dynamic_slice_in_dim(scale_one, tensor_rank * own_rows, own_rows, 0)
    residual = input_own + attn_own
    scale_two = rms_scale(residual)
    ffn_in = (residual * scale_two * ffn_gain).astype(jnp.bfloat16)
    logits = jnp.dot(ffn_in, w_router, preferred_element_type=jnp.float32)
    probabilities = jax.nn.softmax(logits, axis=-1)
    chosen = routes[:, :, None] == jnp.arange(experts_all, dtype=jnp.int32)[None, None, :]
    gate_weights = jnp.sum(jnp.where(chosen, probabilities[:, None, :], 0.0), axis=-1)
    grad_output = cotangent.astype(jnp.float32)
    flat_routes = routes.reshape(-1)
    expert_hits = (
        flat_routes[:, None] == jnp.arange(experts_all, dtype=jnp.int32)[None, :]
    ).astype(jnp.int32)
    slot_index = jnp.sum(expert_hits * (jnp.cumsum(expert_hits, axis=0) - 1), axis=1)
    spread_in = jnp.broadcast_to(ffn_in[:, None, :], (own_rows, top_count, model_width)).reshape(
        -1, model_width
    )
    spread_grad = (
        (gate_weights[:, :, None] * grad_output[:, None, :])
        .astype(jnp.bfloat16)
        .reshape(-1, model_width)
    )
    send_in = (
        jnp.zeros((experts_all, capacity, model_width), jnp.bfloat16)
        .at[flat_routes, slot_index]
        .set(spread_in)
    )
    send_grad = (
        jnp.zeros((experts_all, capacity, model_width), jnp.bfloat16)
        .at[flat_routes, slot_index]
        .set(spread_grad)
    )
    layout = (senders, experts_here, capacity, model_width)
    recv_rows, expert_grad = (
        lax.all_to_all(send_in.reshape(layout), "expert", split_axis=0, concat_axis=0, tiled=True),
        lax.all_to_all(
            send_grad.reshape(layout), "expert", split_axis=0, concat_axis=0, tiled=True
        ),
    )
    gate_full, up_full, down_full = (
        lax.all_gather(w_gate, "tensor", axis=2, tiled=True),
        lax.all_gather(w_up, "tensor", axis=2, tiled=True),
        lax.all_gather(w_down, "tensor", axis=1, tiled=True),
    )
    gate_all = jnp.einsum(
        "sctd,cdf->sctf", recv_rows, gate_full, preferred_element_type=jnp.float32
    )
    up_all = jnp.einsum("sctd,cdf->sctf", recv_rows, up_full, preferred_element_type=jnp.float32)
    hidden_low = (jax.nn.silu(gate_all) * up_all).astype(jnp.bfloat16)
    expert_out = jnp.einsum(
        "sctf,cfd->sctd", hidden_low, down_full, preferred_element_type=jnp.float32
    ).astype(jnp.bfloat16)
    grad_hidden = jnp.einsum(
        "sctd,cfd->sctf", expert_grad, down_full, preferred_element_type=jnp.float32
    )
    grad_gate_pre, grad_up_pre = swiglu_back(grad_hidden, gate_all, up_all)
    whole_down = jnp.einsum(
        "sctf,sctd->cfd", hidden_low, expert_grad, preferred_element_type=jnp.float32
    )
    whole_gate = jnp.einsum(
        "sctd,sctf->cdf", recv_rows, grad_gate_pre, preferred_element_type=jnp.float32
    )
    whole_up = jnp.einsum(
        "sctd,sctf->cdf", recv_rows, grad_up_pre, preferred_element_type=jnp.float32
    )
    from_gate = jnp.einsum(
        "sctf,cdf->sctd", grad_gate_pre, gate_full, preferred_element_type=jnp.float32
    )
    from_up = jnp.einsum("sctf,cdf->sctd", grad_up_pre, up_full, preferred_element_type=jnp.float32)
    grad_inputs = (from_gate + from_up).astype(jnp.bfloat16)
    grad_gate, grad_up, grad_down = (
        lax.psum_scatter(
            whole_gate.astype(jnp.bfloat16), "tensor", scatter_dimension=2, tiled=True
        ).astype(jnp.float32),
        lax.psum_scatter(
            whole_up.astype(jnp.bfloat16), "tensor", scatter_dimension=2, tiled=True
        ).astype(jnp.float32),
        lax.psum_scatter(
            whole_down.astype(jnp.bfloat16), "tensor", scatter_dimension=1, tiled=True
        ).astype(jnp.float32),
    )
    back_rows, back_grads = (
        lax.all_to_all(expert_out, "expert", split_axis=0, concat_axis=0, tiled=True),
        lax.all_to_all(grad_inputs, "expert", split_axis=0, concat_axis=0, tiled=True),
    )
    pick_index = flat_routes * capacity + slot_index
    rows_back = (
        back_rows.reshape(experts_all * capacity, model_width)[pick_index]
        .reshape(own_rows, top_count, model_width)
        .astype(jnp.float32)
    )
    grads_back = (
        back_grads.reshape(experts_all * capacity, model_width)[pick_index]
        .reshape(own_rows, top_count, model_width)
        .astype(jnp.float32)
    )
    mixture = jnp.sum(gate_weights[:, :, None] * rows_back, axis=1)
    output = (residual + mixture).astype(jnp.bfloat16)
    grad_gates = jnp.sum(grad_output[:, None, :] * rows_back, axis=-1)
    grad_probs = jnp.sum(jnp.where(chosen, grad_gates[:, :, None], 0.0), axis=1)
    grad_logits = (
        probabilities * (grad_probs - jnp.sum(grad_probs * probabilities, axis=-1, keepdims=True))
    ).astype(jnp.bfloat16)
    router_part = lax.dot_general(
        ffn_in, grad_logits, (((0,), (0,)), ((), ())), preferred_element_type=jnp.float32
    )
    grad_ffn = jnp.sum(grads_back, axis=1) + lax.dot_general(
        grad_logits, w_router, (((1,), (1,)), ((), ())), preferred_element_type=jnp.float32
    )
    ffn_gain_part = jnp.sum(grad_ffn * residual * scale_two, axis=0)
    scaled_two = grad_ffn * ffn_gain
    grad_residual = grad_output + scale_two * (
        scaled_two
        - residual * scale_two * scale_two * jnp.mean(scaled_two * residual, axis=-1, keepdims=True)
    )
    grad_attn = grad_residual.astype(jnp.bfloat16)
    shard_part = lax.all_gather(grad_attn, "tensor", axis=0, tiled=True)
    grad_weight = lax.dot_general(
        mixed_low, shard_part, (((0,), (0,)), ((), ())), preferred_element_type=jnp.float32
    )
    grad_rows_part = lax.dot_general(
        shard_part, w_out, (((1,), (1,)), ((), ())), preferred_element_type=jnp.float32
    ).astype(jnp.bfloat16)
    grad_mixed = grad_rows_part
    out_part, grad_mixed = (grad_weight, grad_mixed)
    grad_query, grad_keys, grad_values = attend_backward(
        query_low,
        key_low,
        value_low,
        segment,
        grad_mixed.reshape(group_rows, local_heads, head_width),
        log_total,
        block_rows,
        score_scale,
    )
    grad_qkv, q_gain_part, k_gain_part = head_back((grad_query, grad_keys, grad_values))
    grad_qkv_low = grad_qkv.astype(jnp.bfloat16).reshape(group_rows, 3 * local_heads * head_width)
    qkv_part = lax.dot_general(
        normed, grad_qkv_low, (((0,), (0,)), ((), ())), preferred_element_type=jnp.float32
    ).reshape(w_qkv.shape)
    row_part = grad_qkv_low
    grad_normed = lax.psum_scatter(
        lax.dot_general(
            row_part, qkv_weight, (((1,), (1,)), ((), ())), preferred_element_type=jnp.float32
        ).astype(jnp.bfloat16),
        "tensor",
        scatter_dimension=0,
        tiled=True,
    ).astype(jnp.float32)
    attn_gain_part = jnp.sum(grad_normed * input_own * scale_own, axis=0)
    scaled_one = grad_normed * attn_gain
    grad_input = grad_residual + scale_own * (
        scaled_one
        - input_own
        * scale_own
        * scale_own
        * jnp.mean(scaled_one * input_own, axis=-1, keepdims=True)
    )
    grad_qkv_sum, grad_out_sum = (
        lax.psum(qkv_part.astype(jnp.bfloat16), "expert").astype(jnp.float32),
        lax.psum(out_part.astype(jnp.bfloat16), "expert").astype(jnp.float32),
    )
    grad_attn_gain, grad_q_gain, grad_k_gain, grad_ffn_gain, grad_router = lax.psum(
        (attn_gain_part, q_gain_part, k_gain_part, ffn_gain_part, router_part), ("expert", "tensor")
    )
    return (
        output,
        grad_input.astype(jnp.bfloat16),
        grad_attn_gain,
        grad_qkv_sum,
        grad_q_gain,
        grad_k_gain,
        grad_out_sum,
        grad_ffn_gain,
        grad_router,
        grad_gate,
        grad_up,
        grad_down,
    )


def solution(mesh):
    in_specs = (
        P("expert", None),
        P(("expert", "tensor"), None),
        P("expert", None),
        P(("expert", "tensor"), None),
        P(),
        P(None, None, "tensor"),
        P(),
        P(),
        P("tensor", None),
        P(),
        P(),
        P("expert", None, "tensor"),
        P("expert", None, "tensor"),
        P("expert", "tensor", None),
    )
    out_specs = (
        P(("expert", "tensor"), None),
        P(("expert", "tensor"), None),
        P(),
        P(None, None, "tensor"),
        P(),
        P(),
        P("tensor", None),
        P(),
        P(),
        P("expert", None, "tensor"),
        P("expert", None, "tensor"),
        P("expert", "tensor", None),
    )
    return jax.shard_map(body, mesh=mesh, in_specs=in_specs, out_specs=out_specs, check_vma=False)
```

profile of v0, /device:TPU:0, one launch (start us, length us, event | category | flops | bytes accessed | tf_op | source)
XLA Modules:
  0.0 2259.6 jit_solution(2812571986861035458)
XLA Ops:
  49.6 41.2 %while.27 = (s32[]{:T(128)}, bf16[4,512,2,128]{3,1,2,0:T(8,128)(2,1)}, f32[4,2,512]{2,1,0:T(2,128)}, s32[4,512]{1,0:T(4,128)S(1)}, s32[2048]{0:T(1024)S(1)}, /*i...) while((s32[]{:T(128)}, ...), condition=%wide.region_9.10_spmd, body=%wide.region_6.9_spmd.sunk | while | flops 1099955200 | bytes 32292448 | solution.py:79
  125.6 96.5 %reduce-scatter.10.cloned.1.call-done = f32[256,2048]{1,0:T(8,128)} async-done(((f32[2048,2048]{1,0:T(8,128)}), f32[256,2048]{1,0:T(8,128)}) %reduce-scatter.10.cloned.1.call-update) | async-done | bytes 2097168 | tf_op jit(solution)/shard_map/reduce_scatter | solution.py:184
  277.0 247.9 %all-to-all-done = bf16[4,4,192,2048]{3,2,1,0:T(8,128)(2,1)} async-done(((bf16[4,4,192,2048]{3,2,1,0:T(8,128)(2,1)}), bf16[4,4,192,2048]{3,2,1,0:T(8,128)(2,1)}, u32[]{:S(2)}, u32[]{:S(2)}) %all-to-all-start) | async-done | bytes 12582944 | tf_op jit(solution)/shard_map/all_to_all | solution.py:225
  531.7 22.6 %fusion.42 = f32[4,4,192,1024]{3,2,1,0:T(8,128)} fusion(bf16[4,2048,1024]{2,1,0:T(8,128)(2,1)} %all-gather.5.cloned.1.call-done, bf16[4,4,192,2048]{3,2,1,0:T(8,128)(2,1)} %all-to-all-done), kind=kOutput, calls=%fused_computation.64 | convolution fusion | flops 12884901888 | bytes 41943040 | tf_op jit(solution)/shard_map/sctd,cdf->sctf/dot_general | solution.py:235
  554.4 22.6 %fusion.38 = f32[4,4,192,1024]{3,2,1,0:T(8,128)} fusion(bf16[4,2048,1024]{2,1,0:T(8,128)(2,1)} %all-gather.7.cloned.1.call-done, bf16[4,4,192,2048]{3,2,1,0:T(8,128)(2,1)} %all-to-all-done), kind=kOutput, calls=%fused_computation.60 | convolution fusion | flops 12884901888 | bytes 41943040 | tf_op jit(solution)/shard_map/sctd,cdf->sctf/dot_general | solution.py:238
  577.0 227.2 %all-to-all-done.2 = bf16[4,4,192,2048]{3,2,1,0:T(8,128)(2,1)} async-done(((bf16[4,4,192,2048]{3,2,1,0:T(8,128)(2,1)}), bf16[4,4,192,2048]{3,2,1,0:T(8,128)(2,1)}, u32[]{:S(2)}, u32[]{:S(2)}) %all-to-all-start.2) | async-done | bytes 12582944 | tf_op jit(solution)/shard_map/all_to_all | solution.py:226
  804.2 31.3 %fusion.52 = (bf16[4,4,192,1024]{3,2,0,1:T(8,128)(2,1)}, bf16[4,4,192,1024]{3,2,0,1:T(8,128)(2,1)}, bf16[4,4,192,1024]{3,2,0,1:T(8,128)(2,1)}) fusion(f32[4,4,192,1024]{3,2,1,0:T(8,128)} %fusion.38, f32[4,4,192,1024]{3,2,1,0:T(8,128)} %fusion.42, bf16[4,1024,2048]{2,1,0:T(8,128)(2,1)} %all-gather.9.cloned.1.call-done, ...), kind=kOutput, calls=%fused_computation.79 | convolution fusion | flops 12935233536 | bytes 73400320 | tf_op jit(solution)/shard_map/sctd,cfd->sctf/dot_general | solution.py:243
  835.5 22.9 %convert_bitcast_fusion = bf16[4,4,192,2048]{3,2,0,1:T(8,128)(2,1)} fusion(bf16[4,4,192,1024]{3,2,0,1:T(8,128)(2,1)} %get-tuple-element.315, bf16[4,1024,2048]{2,1,0:T(8,128)(2,1)} %all-gather.9.cloned.1.call-done), kind=kOutput, calls=%fused_computation.91 | convolution fusion | flops 12891193344 | bytes 35651584 | tf_op jit(solution)/shard_map/sctf,cfd->sctd/dot_general | solution.py:240
  875.5 21.8 fusion.36
  897.3 24.3 %fusion.49 = bf16[4,4,192,2048]{3,2,0,1:T(8,128)(2,1)} fusion(f32[4,4,192,2048]{3,2,1,0:T(8,128)} %fusion.36, bf16[4,4,192,1024]{3,2,0,1:T(8,128)(2,1)} %get-tuple-element.314, bf16[4,2048,1024]{2,1,0:T(8,128)(2,1)} %all-gather.5.cloned.1.call-done), kind=kOutput, calls=%fused_computation.74 | convolution fusion | flops 12897484800 | bytes 60817408 | tf_op jit(solution)/shard_map/sctf,cdf->sctd/dot_general | solution.py:256
  932.3 215.7 %all-to-all-done.1 = bf16[4,4,192,2048]{3,2,1,0:T(8,128)(2,1)} async-done(((bf16[4,4,192,2048]{3,2,1,0:T(8,128)(2,1)}), bf16[4,4,192,2048]{3,2,1,0:T(8,128)(2,1)}, u32[]{:S(2)}, u32[]{:S(2)}) %all-to-all-start.1) | async-done | bytes 12582944 | tf_op jit(solution)/shard_map/all_to_all | solution.py:273
  1154.4 22.9 %gather_fusion = bf16[2048,2048]{1,0:T(8,128)(2,1)} fusion(bf16[3072,2048]{1,0:T(8,128)(2,1)} %bitcast.30, s32[2048]{0:T(1024)S(1)} %broadcast_clamp_fusion), kind=kCustom, calls=%fused_computation | custom fusion | bytes 16785408 | tf_op jit(solution)/shard_map/gather | solution.py:278
  1187.0 239.8 %all-to-all-done.3 = bf16[4,4,192,2048]{3,2,1,0:T(8,128)(2,1)} async-done(((bf16[4,4,192,2048]{3,2,1,0:T(8,128)(2,1)}), bf16[4,4,192,2048]{3,2,1,0:T(8,128)(2,1)}, u32[]{:S(2)}, u32[]{:S(2)}) %all-to-all-start.3) | async-done | bytes 12582944 | tf_op jit(solution)/shard_map/all_to_all | solution.py:274
  1426.8 22.9 %gather_fusion.1 = bf16[2048,2048]{1,0:T(8,128)(2,1)} fusion(bf16[3072,2048]{1,0:T(8,128)(2,1)} %bitcast.40, s32[2048]{0:T(1024)S(1)} %broadcast_clamp_fusion), kind=kCustom, calls=%fused_computation.1 | custom fusion | bytes 16785408 | tf_op jit(solution)/shard_map/gather | solution.py:283
  1487.2 28.9 %copy.149 = bf16[4,2048,1024]{1,0,2:T(4,128)(2,1)} copy(bf16[4,2048,1024]{2,1,0:T(8,128)(2,1)} %bitcast_convert_fusion.2) | data formatting | bytes 33554432
  1534.7 20.5 bitcast_convert_fusion.1
  1555.2 29.2 %copy.151 = bf16[4,2048,1024]{1,0,2:T(4,128)(2,1)} copy(bf16[4,2048,1024]{2,1,0:T(8,128)(2,1)} %bitcast_convert_fusion.1) | data formatting | bytes 33554432
  1603.4 21.6 bitcast_convert_fusion
  1632.1 165.0 %while.28 = (s32[]{:T(128)}, f32[2048,2,128]{0,2,1:T(8,128)}, f32[2048,2,128]{0,2,1:T(8,128)}, f32[4,512,2,128]{1,0,3,2:T(4,128)}, bf16[4,512,2,128]{3,1,2,0:T(8...) while((s32[]{:T(128)}, f32[2048,2,128]{0,2,1:T(8,128)}, ...), condition=%wide.region_28.29_spmd.clone, body=%wide.region_26.28_spmd.clone.sunk | while | flops 2719611904 | bytes 170962192 | solution.py:125
  1859.3 29.5 %reduce-scatter.14.cloned.1.call-done = bf16[4,128,2048]{2,1,0:T(8,128)(2,1)} async-done(((bf16[4,1024,2048]{2,1,0:T(8,128)(2,1)}), bf16[4,128,2048]{2,1,0:T(8,128)(2,1)}) %reduce-scatter.14.cloned.1.call-update) | async-done | bytes 2097168 | tf_op jit(solution)/shard_map/reduce_scatter | solution.py:268
  1892.9 153.9 %all-reduce.14.cloned.1.call-done = (bf16[2048,3,256]{2,0,1:T(8,128)(2,1)}, bf16[256,2048]{1,0:T(8,128)(2,1)}) async-done(((bf16[2048,3,256]{2,0,1:T(8,128)(2,1)}, bf16[256,2048]{1,0:T(8,128)(2,1)}), (bf16[2048,3,256]{2,0,1:T(8,128)(2,1)}, bf16[256,2048]{1,0:T(8,128)(2,1)})) %all-reduce.14.cloned.1.call-update) | async-done | bytes 4194320 | tf_op jit(solution)/shard_map/psum | solution.py:350
  2053.7 67.0 %reduce-scatter.12.cloned.1.call-done = bf16[256,2048]{1,0:T(8,128)(2,1)} async-done(((bf16[2048,2048]{1,0:T(8,128)(2,1)}), bf16[256,2048]{1,0:T(8,128)(2,1)}) %reduce-scatter.12.cloned.1.call-update) | async-done | bytes 1048592 | tf_op jit(solution)/shard_map/reduce_scatter | solution.py:332
  2129.3 39.8 %all-reduce.7 = (f32[2048]{0:T(1024)}, f32[128]{0:T(128)}, f32[128]{0:T(128)}, f32[2048]{0:T(1024)}) all-reduce(f32[2048]{0:T(1024)S(1)} %get-tuple-element.250, f32[128]{0:T(128)S(1)} %get-tuple-element.259, f32[128]{0:T(128)S(1)} %get-tuple-element.252, ...), channel_id=1, replica_groups=mesh['expert'=4,'tensor'=8] {'expert','tensor'}, use_global_device_ids=true, to_apply=%region_34.35 | all-reduce | flops 4352 | bytes 34816 | tf_op jit(solution)/shard_map/psum | solution.py:353
  2169.0 82.2 %all-reduce.12.cloned.1.call-done = f32[2048,16]{0,1:T(8,128)} async-done(((f32[2048,16]{0,1:T(8,128)}), f32[2048,16]{0,1:T(8,128)}) %all-reduce.12.cloned.1.call-update) | async-done | bytes 131088 | tf_op jit(solution)/shard_map/psum | solution.py:353
  (384 shorter events, 552.6 us)
Async XLA Ops:
  7.2 87.8 %copy-start = (bf16[256,2048]{1,0:T(8,128)(2,1)S(1)}, bf16[256,2048]{1,0:T(8,128)(2,1)}, u32[]{:S(2)}) copy-start(bf16[256,2048]{1,0:T(8,128)(2,1)} %param.26) | copy-start | bytes 3145732
  7.2 215.0 %reduce-scatter.10.cloned.1.call-start = ((), (), s32[]{:S(2)}) async-start(), calls=%async_computation.9 | async-start | bytes 18874368 | tf_op jit(solution)/shard_map/reduce_scatter | solution.py:184
  103.1 428.6 %all-gather.5.cloned.1.call-start = ((), (), s32[]{:S(2)}) async-start(), calls=%async_computation.10 | async-start | bytes 18874368 | tf_op jit(solution)/shard_map/all_gather | solution.py:231
  103.9 450.5 %all-gather.7.cloned.1.call-start = ((), (), s32[]{:S(2)}) async-start(), calls=%async_computation.11 | async-start | bytes 18874368 | tf_op jit(solution)/shard_map/all_gather | solution.py:232
  118.8 107.3 %copy-start.40 = (f32[2048]{0:T(1024)S(1)}, f32[2048]{0:T(1024)}, u32[]{:S(2)}) copy-start(f32[2048]{0:T(1024)} %param.27) | copy-start | bytes 24580
  245.4 279.5 %all-to-all-start = ((bf16[4,4,192,2048]{3,2,1,0:T(8,128)(2,1)}), bf16[4,4,192,2048]{3,2,1,0:T(8,128)(2,1)}, u32[]{:S(2)}, u32[]{:S(2)}) async-start(bf16[4,4,192,2048]{3,2,1,0:T(8,128)(2,1)} %bitcast.307), calls=%async_computation.1 | async-start | bytes 25165824 | tf_op jit(solution)/shard_map/all_to_all | solution.py:225
  251.8 325.1 %all-gather.9.cloned.1.call-start = ((), (), s32[]{:S(2)}) async-start(), calls=%async_computation.12 | async-start | bytes 18874368 | tf_op jit(solution)/shard_map/all_gather | solution.py:233
  253.9 23.1 %copy-start.13 = (f32[256,2048]{1,0:T(8,128)}, f32[256,2048]{1,0:T(8,128)S(1)}, u32[]{:S(2)}) copy-start(f32[256,2048]{1,0:T(8,128)S(1)} %convert_element_type.161) | copy-start | bytes 6291460
  524.9 279.3 %all-to-all-start.2 = ((bf16[4,4,192,2048]{3,2,1,0:T(8,128)(2,1)}), bf16[4,4,192,2048]{3,2,1,0:T(8,128)(2,1)}, u32[]{:S(2)}, u32[]{:S(2)}) async-start(bf16[4,4,192,2048]{3,2,1,0:T(8,128)(2,1)} %bitcast.308), calls=%async_computation.3 | async-start | bytes 25165824 | tf_op jit(solution)/shard_map/all_to_all | solution.py:226
  869.2 278.8 %all-to-all-start.1 = ((bf16[4,4,192,2048]{3,2,1,0:T(8,128)(2,1)}), bf16[4,4,192,2048]{3,2,1,0:T(8,128)(2,1)}, u32[]{:S(2)}, u32[]{:S(2)}) async-start(bf16[4,4,192,2048]{3,2,1,0:T(8,128)(2,1)} %copy.127), calls=%async_computation.2 | async-start | bytes 25165824 | tf_op jit(solution)/shard_map/all_to_all | solution.py:273
  932.3 222.1 %copy-start.51 = (s32[2048,1]{0,1:T(1,128)S(1)}, s32[2048,1]{0,1:T(1,128)}, u32[]{:S(2)}) copy-start(s32[2048,1]{0,1:T(1,128)} %get-tuple-element.337) | copy-start | bytes 24580
  1148.0 278.8 %all-to-all-start.3 = ((bf16[4,4,192,2048]{3,2,1,0:T(8,128)(2,1)}), bf16[4,4,192,2048]{3,2,1,0:T(8,128)(2,1)}, u32[]{:S(2)}, u32[]{:S(2)}) async-start(bf16[4,4,192,2048]{3,2,1,0:T(8,128)(2,1)} %copy.130), calls=%async_computation.4 | async-start | bytes 25165824 | tf_op jit(solution)/shard_map/all_to_all | solution.py:274
  1154.3 470.8 %all-gather.11.cloned.1.call-start = ((), (), s32[]{:S(2)}) async-start(), calls=%async_computation.13 | async-start | bytes 9437184 | tf_op jit(solution)/shard_map/all_gather | solution.py:307
  1187.0 274.3 %copy-start.44 = (bf16[256,16]{0,1:T(8,128)(2,1)}, bf16[256,16]{0,1:T(8,128)(2,1)S(1)}, u32[]{:S(2)}) copy-start(bf16[256,16]{0,1:T(8,128)(2,1)S(1)} %multiply_convert_fusion.5) | copy-start | bytes 24580
  1467.4 371.4 %reduce-scatter.16.cloned.1.call-start = ((), (), s32[]{:S(2)}) async-start(), calls=%async_computation.17 | async-start | bytes 18874368
  1534.7 314.4 %reduce-scatter.18.cloned.1.call-start = ((), (), s32[]{:S(2)}) async-start(), calls=%async_computation.18 | async-start | bytes 18874368
  1603.4 285.4 %reduce-scatter.14.cloned.1.call-start = ((), (), s32[]{:S(2)}) async-start(), calls=%async_computation.16 | async-start | bytes 18874368 | tf_op jit(solution)/shard_map/reduce_scatter | solution.py:268
  1625.0 421.8 %all-reduce.14.cloned.1.call-start = ((), (), s32[]{:S(2)}) async-start(), calls=%async_computation.19 | async-start | bytes 8388608 | tf_op jit(solution)/shard_map/psum | solution.py:350
  1824.8 295.9 %reduce-scatter.12.cloned.1.call-start = ((), (), s32[]{:S(2)}) async-start(), calls=%async_computation.14 | async-start | bytes 9437184 | tf_op jit(solution)/shard_map/reduce_scatter | solution.py:332
  1836.6 414.6 %all-reduce.12.cloned.1.call-start = ((), (), s32[]{:S(2)}) async-start(), calls=%async_computation.15 | async-start | bytes 262144 | tf_op jit(solution)/shard_map/psum | solution.py:353
  2046.8 76.4 %copy-start.8 = (f32[256,2048]{1,0:T(8,128)S(1)}, f32[256,2048]{1,0:T(8,128)}, u32[]{:S(2)}) copy-start(f32[256,2048]{1,0:T(8,128)} %copy-done.6) | copy-start | bytes 6291460
  2046.8 76.4 %copy-start.42 = (f32[2048]{0:T(1024)S(1)}, f32[2048]{0:T(1024)}, u32[]{:S(2)}) copy-start(f32[2048]{0:T(1024)} %param.27) | copy-start | bytes 24580
  2046.8 76.4 %copy-start.54 = (f32[256]{0:T(256)S(1)}, f32[256]{0:T(256)}, u32[]{:S(2)}) copy-start(f32[256]{0:T(256)} %copy-done.52) | copy-start | bytes 3076
  2046.8 76.4 %copy-start.62 = (f32[256]{0:T(256)S(1)}, f32[256]{0:T(256)}, u32[]{:S(2)}) copy-start(f32[256]{0:T(256)} %copy-done.61) | copy-start | bytes 3076
  (79 other events, 612.5 us)
Sparse Core Ops, SparseCore 0:
  103.2 118.8 reduce-scatter.9
  224.0 93.0 all-gather.4
  319.0 93.0 all-gather.6
  413.8 89.7 all-gather.8
  1467.5 52.3 all-gather.10
  1534.8 114.4 reduce-scatter.15
  1652.8 116.1 reduce-scatter.17
  1772.6 116.1 reduce-scatter.13
  1891.8 154.9 all-reduce.13
  2050.1 70.4 reduce-scatter.11
  2126.8 124.4 all-reduce.11
where the time goes:
time: 2270 us; the launch traced here: 2260 us
  waiting for transfers between devices  1360 us (60%)
  matrix products  361 us (16%)
  local copies, waits for them, and re-layouts  310 us (14%)
  other arithmetic  145 us (6%)
  blocking collectives  39.8 us (2%)
  starting transfers between devices  26.5 us (1%)
    all_to_all x1, waiting for transfers between devices, body(): lax.all_to_all(send_in.reshape(layout), 'expert', split_axis=0, concat_ax...  248 us
    all_to_all x1, waiting for transfers between devices, body(): lax.all_to_all(grad_inputs, 'expert', split_axis=0, concat_axis=0, tiled=...  240 us
    all_to_all x1, waiting for transfers between devices, body(): lax.all_to_all(send_grad.reshape(layout), 'expert', split_axis=0, concat_...  227 us
    all_to_all x1, waiting for transfers between devices, body(): lax.all_to_all(expert_out, 'expert', split_axis=0, concat_axis=0, tiled=T...  216 us
    psum x1, waiting for transfers between devices, body(): lax.psum(qkv_part.astype(jnp.bfloat16), 'expert').astype(jnp.float32)  154 us
    unnamed x156, local copies, waits for them, and re-layouts  146 us
    reduce_scatter x1, waiting for transfers between devices, body(): lax.psum_scatter(jnp.dot(row_part, w_out, preferred_element_type=jnp.floa...  96.5 us
    psum x1, waiting for transfers between devices, body(): lax.psum((attn_gain_part, q_gain_part, k_gain_part, ffn_gain_part, router...  82.2 us
  transfers between devices with their start and end apart: 15, of which 9 were waited for; matrix products, arithmetic and copies ran while one was open for 26% of the time, Pallas kernels for 0%

commit v1 on v0

--- a/solution.py
+++ b/solution.py
@@ -347,7 +347,9 @@
         * jnp.mean(scaled_one * input_own, axis=-1, keepdims=True)
     )
     grad_qkv_sum, grad_out_sum = (
-        lax.psum(qkv_part.astype(jnp.bfloat16), "expert").astype(jnp.float32),
+        jax.lax.all_gather(qkv_part.astype(jnp.bfloat16), axis_name="expert")
+        .sum(axis=0)
+        .astype(jnp.float32),
         lax.psum(out_part.astype(jnp.bfloat16), "expert").astype(jnp.float32),
     )
     grad_attn_gain, grad_q_gain, grad_k_gain, grad_ffn_gain, grad_router = lax.psum(

time: 2270 us -> 2390 us (1.053)
  waiting for transfers between devices: 1360 us -> 1450 us
    all_gather x0 -> x1, waiting for transfers between devices: none -> 159 us  [body(): jax.lax.all_gather(qkv_part.astype(jnp.bfloat16), axis_name='expert')]
    psum x1, waiting for transfers between devices: 154 us -> 50.8 us  [body(): lax.psum(out_part.astype(jnp.bfloat16), 'expert').astype(jnp.float32)]
    psum x1, waiting for transfers between devices: 82.2 us -> 115 us  [body(): lax.psum((attn_gain_part, q_gain_part, k_gain_part, ffn_gain_part, router...]
    unnamed x156 -> x150, local copies, waits for them, and re-layouts: 146 us -> 146 us
  transfers between devices with their start and end apart: 15 -> 16, of which waited for: 9 -> 10; matrix products, arithmetic and copies ran while one was open for 26% -> 26% of each run, Pallas kernels for 0% -> 0%
where the time goes in v1:
time: 2390 us; the launch traced here: 2380 us
  waiting for transfers between devices  1450 us (61%)
  matrix products  366 us (15%)
  local copies, waits for them, and re-layouts  310 us (13%)
  other arithmetic  154 us (6%)
  blocking collectives  53.8 us (2%)
  starting transfers between devices  26.8 us (1%)
    all_to_all x1, waiting for transfers between devices, body(): lax.all_to_all(send_in.reshape(layout), 'expert', split_axis=0, concat_ax...  248 us
    all_to_all x1, waiting for transfers between devices, body(): lax.all_to_all(grad_inputs, 'expert', split_axis=0, concat_axis=0, tiled=...  240 us
    all_to_all x1, waiting for transfers between devices, body(): lax.all_to_all(send_grad.reshape(layout), 'expert', split_axis=0, concat_...  227 us
    all_to_all x1, waiting for transfers between devices, body(): lax.all_to_all(expert_out, 'expert', split_axis=0, concat_axis=0, tiled=T...  216 us
    all_gather x1, waiting for transfers between devices, body(): jax.lax.all_gather(qkv_part.astype(jnp.bfloat16), axis_name='expert')  159 us
    unnamed x150, local copies, waits for them, and re-layouts  146 us
    psum x1, waiting for transfers between devices, body(): lax.psum((attn_gain_part, q_gain_part, k_gain_part, ffn_gain_part, router...  115 us
    reduce_scatter x1, waiting for transfers between devices, body(): lax.psum_scatter(jnp.dot(row_part, w_out, preferred_element_type=jnp.floa...  96.5 us
  transfers between devices with their start and end apart: 16, of which 10 were waited for; matrix products, arithmetic and copies ran while one was open for 26% of the time, Pallas kernels for 0%

profile of v1, /device:TPU:0, one launch (start us, length us, event | category | flops | bytes accessed | tf_op | source)
XLA Modules:
  0.0 2375.7 jit_solution(16182679362215101487)
XLA Ops:
  49.7 41.0 %while.27 = (s32[]{:T(128)}, bf16[4,512,2,128]{3,1,2,0:T(8,128)(2,1)}, f32[4,2,512]{2,1,0:T(2,128)}, s32[4,512]{1,0:T(4,128)S(1)}, s32[2048]{0:T(1024)S(1)}, /*i...) while((s32[]{:T(128)}, ...), condition=%wide.region_9.10_spmd, body=%wide.region_6.9_spmd.sunk | while | flops 1099955200 | bytes 32292448 | solution.py:79
  125.4 96.5 %reduce-scatter.10.cloned.1.call-done = f32[256,2048]{1,0:T(8,128)} async-done(((f32[2048,2048]{1,0:T(8,128)}), f32[256,2048]{1,0:T(8,128)}) %reduce-scatter.10.cloned.1.call-update) | async-done | bytes 2097168 | tf_op jit(solution)/shard_map/reduce_scatter | solution.py:184
  276.7 247.9 %all-to-all-done = bf16[4,4,192,2048]{3,2,1,0:T(8,128)(2,1)} async-done(((bf16[4,4,192,2048]{3,2,1,0:T(8,128)(2,1)}), bf16[4,4,192,2048]{3,2,1,0:T(8,128)(2,1)}, u32[]{:S(2)}, u32[]{:S(2)}) %all-to-all-start) | async-done | bytes 12582944 | tf_op jit(solution)/shard_map/all_to_all | solution.py:225
  531.2 22.6 fusion.42
  553.7 22.5 fusion.38
  576.3 227.4 %all-to-all-done.2 = bf16[4,4,192,2048]{3,2,1,0:T(8,128)(2,1)} async-done(((bf16[4,4,192,2048]{3,2,1,0:T(8,128)(2,1)}), bf16[4,4,192,2048]{3,2,1,0:T(8,128)(2,1)}, u32[]{:S(2)}, u32[]{:S(2)}) %all-to-all-start.2) | async-done | bytes 12582944 | tf_op jit(solution)/shard_map/all_to_all | solution.py:226
  803.6 31.3 %fusion.52 = (bf16[4,4,192,1024]{3,2,0,1:T(8,128)(2,1)}, bf16[4,4,192,1024]{3,2,0,1:T(8,128)(2,1)}, bf16[4,4,192,1024]{3,2,0,1:T(8,128)(2,1)}) fusion(f32[4,4,192,1024]{3,2,1,0:T(8,128)} %fusion.38, f32[4,4,192,1024]{3,2,1,0:T(8,128)} %fusion.42, bf16[4,1024,2048]{2,1,0:T(8,128)(2,1)} %all-gather.11.cloned.1.call-done, ...), kind=kOutput, calls=%fused_computation.79 | convolution fusion | flops 12935233536 | bytes 73400320 | tf_op jit(solution)/shard_map/sctd,cfd->sctf/dot_general | solution.py:243
  834.9 23.0 convert_bitcast_fusion
  874.9 21.8 fusion.36
  896.7 24.3 %fusion.49 = bf16[4,4,192,2048]{3,2,0,1:T(8,128)(2,1)} fusion(f32[4,4,192,2048]{3,2,1,0:T(8,128)} %fusion.36, bf16[4,4,192,1024]{3,2,0,1:T(8,128)(2,1)} %get-tuple-element.312, bf16[4,2048,1024]{2,1,0:T(8,128)(2,1)} %all-gather.7.cloned.1.call-done), kind=kOutput, calls=%fused_computation.74 | convolution fusion | flops 12897484800 | bytes 60817408 | tf_op jit(solution)/shard_map/sctf,cdf->sctd/dot_general | solution.py:256
  931.7 215.7 %all-to-all-done.1 = bf16[4,4,192,2048]{3,2,1,0:T(8,128)(2,1)} async-done(((bf16[4,4,192,2048]{3,2,1,0:T(8,128)(2,1)}), bf16[4,4,192,2048]{3,2,1,0:T(8,128)(2,1)}, u32[]{:S(2)}, u32[]{:S(2)}) %all-to-all-start.1) | async-done | bytes 12582944 | tf_op jit(solution)/shard_map/all_to_all | solution.py:273
  1153.8 23.1 gather_fusion
  1186.6 239.7 %all-to-all-done.3 = bf16[4,4,192,2048]{3,2,1,0:T(8,128)(2,1)} async-done(((bf16[4,4,192,2048]{3,2,1,0:T(8,128)(2,1)}), bf16[4,4,192,2048]{3,2,1,0:T(8,128)(2,1)}, u32[]{:S(2)}, u32[]{:S(2)}) %all-to-all-start.3) | async-done | bytes 12582944 | tf_op jit(solution)/shard_map/all_to_all | solution.py:274
  1426.3 22.7 gather_fusion.1
  1486.4 28.9 %copy.149 = bf16[4,2048,1024]{1,0,2:T(4,128)(2,1)} copy(bf16[4,2048,1024]{2,1,0:T(8,128)(2,1)} %bitcast_convert_fusion.2) | data formatting | bytes 33554432
  1554.3 29.2 %copy.151 = bf16[4,2048,1024]{1,0,2:T(4,128)(2,1)} copy(bf16[4,2048,1024]{2,1,0:T(8,128)(2,1)} %bitcast_convert_fusion.1) | data formatting | bytes 33554432
  1602.5 21.8 bitcast_convert_fusion
  1631.4 165.0 %while.28 = (s32[]{:T(128)}, f32[2048,2,128]{0,2,1:T(8,128)}, f32[2048,2,128]{0,2,1:T(8,128)}, f32[4,512,2,128]{1,0,3,2:T(4,128)}, bf16[4,512,2,128]{3,1,2,0:T(8...) while((s32[]{:T(128)}, f32[2048,2,128]{0,2,1:T(8,128)}, ...), condition=%wide.region_28.29_spmd.clone, body=%wide.region_26.28_spmd.clone.sunk | while | flops 2719611904 | bytes 170962192 | solution.py:125
  1862.8 25.3 %reduce-scatter.14.cloned.1.call-done = bf16[4,128,2048]{2,1,0:T(8,128)(2,1)} async-done(((bf16[4,1024,2048]{2,1,0:T(8,128)(2,1)}), bf16[4,128,2048]{2,1,0:T(8,128)(2,1)}) %reduce-scatter.14.cloned.1.call-update) | async-done | bytes 2097168 | tf_op jit(solution)/shard_map/reduce_scatter | solution.py:268
  1892.2 50.8 %all-reduce.11.cloned.1.call-done = bf16[256,2048]{1,0:T(8,128)(2,1)} async-done(((bf16[256,2048]{1,0:T(8,128)(2,1)}), bf16[256,2048]{1,0:T(8,128)(2,1)}) %all-reduce.11.cloned.1.call-update) | async-done | bytes 1048592 | tf_op jit(solution)/shard_map/psum | solution.py:353
  1945.8 71.3 %reduce-scatter.12.cloned.1.call-done = bf16[256,2048]{1,0:T(8,128)(2,1)} async-done(((bf16[2048,2048]{1,0:T(8,128)(2,1)}), bf16[256,2048]{1,0:T(8,128)(2,1)}) %reduce-scatter.12.cloned.1.call-update) | async-done | bytes 1048592 | tf_op jit(solution)/shard_map/reduce_scatter | solution.py:332
  2025.8 53.8 %all-reduce.7 = (f32[2048]{0:T(1024)}, f32[128]{0:T(128)}, f32[128]{0:T(128)}, f32[2048]{0:T(1024)}) all-reduce(f32[2048]{0:T(1024)S(1)} %get-tuple-element.250, f32[128]{0:T(128)S(1)} %get-tuple-element.259, f32[128]{0:T(128)S(1)} %get-tuple-element.252, ...), channel_id=1, replica_groups=mesh['expert'=4,'tensor'=8] {'expert','tensor'}, use_global_device_ids=true, to_apply=%region_34.35 | all-reduce | flops 4352 | bytes 34816 | tf_op jit(solution)/shard_map/psum | solution.py:355
  2079.5 158.9 %all-gather.15.cloned.1.call-done = bf16[8192,3,256]{2,0,1:T(8,128)(2,1)} async-done(((bf16[2048,3,256]{2,0,1:T(8,128)(2,1)}), bf16[8192,3,256]{2,0,1:T(8,128)(2,1)}) %all-gather.15.cloned.1.call-update) | async-done | bytes 12582928 | tf_op jit(solution)/shard_map/all_gather | solution.py:350
  2252.6 114.5 %all-reduce.13.cloned.1.call-done = f32[2048,16]{0,1:T(8,128)} async-done(((f32[2048,16]{0,1:T(8,128)}), f32[2048,16]{0,1:T(8,128)}) %all-reduce.13.cloned.1.call-update) | async-done | bytes 131088 | tf_op jit(solution)/shard_map/psum | solution.py:355
  (380 shorter events, 586.9 us)
Async XLA Ops:
  7.2 87.6 %copy-start = (bf16[256,2048]{1,0:T(8,128)(2,1)S(1)}, bf16[256,2048]{1,0:T(8,128)(2,1)}, u32[]{:S(2)}) copy-start(bf16[256,2048]{1,0:T(8,128)(2,1)} %param.26) | copy-start | bytes 3145732
  7.2 214.7 %reduce-scatter.10.cloned.1.call-start = ((), (), s32[]{:S(2)}) async-start(), calls=%async_computation.9 | async-start | bytes 18874368 | tf_op jit(solution)/shard_map/reduce_scatter | solution.py:184
  102.9 428.3 %all-gather.7.cloned.1.call-start = ((), (), s32[]{:S(2)}) async-start(), calls=%async_computation.10 | async-start | bytes 18874368 | tf_op jit(solution)/shard_map/all_gather | solution.py:231
  103.6 450.1 %all-gather.9.cloned.1.call-start = ((), (), s32[]{:S(2)}) async-start(), calls=%async_computation.11 | async-start | bytes 18874368 | tf_op jit(solution)/shard_map/all_gather | solution.py:232
  118.5 107.3 %copy-start.41 = (f32[2048]{0:T(1024)S(1)}, f32[2048]{0:T(1024)}, u32[]{:S(2)}) copy-start(f32[2048]{0:T(1024)} %param.27) | copy-start | bytes 24580
  245.1 279.5 %all-to-all-start = ((bf16[4,4,192,2048]{3,2,1,0:T(8,128)(2,1)}), bf16[4,4,192,2048]{3,2,1,0:T(8,128)(2,1)}, u32[]{:S(2)}, u32[]{:S(2)}) async-start(bf16[4,4,192,2048]{3,2,1,0:T(8,128)(2,1)} %bitcast.308), calls=%async_computation.1 | async-start | bytes 25165824 | tf_op jit(solution)/shard_map/all_to_all | solution.py:225
  251.5 324.7 %all-gather.11.cloned.1.call-start = ((), (), s32[]{:S(2)}) async-start(), calls=%async_computation.12 | async-start | bytes 18874368 | tf_op jit(solution)/shard_map/all_gather | solution.py:233
  524.6 279.0 %all-to-all-start.2 = ((bf16[4,4,192,2048]{3,2,1,0:T(8,128)(2,1)}), bf16[4,4,192,2048]{3,2,1,0:T(8,128)(2,1)}, u32[]{:S(2)}, u32[]{:S(2)}) async-start(bf16[4,4,192,2048]{3,2,1,0:T(8,128)(2,1)} %bitcast.309), calls=%async_computation.3 | async-start | bytes 25165824 | tf_op jit(solution)/shard_map/all_to_all | solution.py:226
  868.6 278.8 %all-to-all-start.1 = ((bf16[4,4,192,2048]{3,2,1,0:T(8,128)(2,1)}), bf16[4,4,192,2048]{3,2,1,0:T(8,128)(2,1)}, u32[]{:S(2)}, u32[]{:S(2)}) async-start(bf16[4,4,192,2048]{3,2,1,0:T(8,128)(2,1)} %copy.127), calls=%async_computation.2 | async-start | bytes 25165824 | tf_op jit(solution)/shard_map/all_to_all | solution.py:273
  931.7 222.1 %copy-start.52 = (s32[2048,1]{0,1:T(1,128)S(1)}, s32[2048,1]{0,1:T(1,128)}, u32[]{:S(2)}) copy-start(s32[2048,1]{0,1:T(1,128)} %get-tuple-element.335) | copy-start | bytes 24580
  1147.4 278.8 %all-to-all-start.3 = ((bf16[4,4,192,2048]{3,2,1,0:T(8,128)(2,1)}), bf16[4,4,192,2048]{3,2,1,0:T(8,128)(2,1)}, u32[]{:S(2)}, u32[]{:S(2)}) async-start(bf16[4,4,192,2048]{3,2,1,0:T(8,128)(2,1)} %copy.130), calls=%async_computation.4 | async-start | bytes 25165824 | tf_op jit(solution)/shard_map/all_to_all | solution.py:274
  1153.7 470.7 %all-gather.13.cloned.1.call-start = ((), (), s32[]{:S(2)}) async-start(), calls=%async_computation.13 | async-start | bytes 9437184 | tf_op jit(solution)/shard_map/all_gather | solution.py:307
  1186.6 273.8 %copy-start.45 = (bf16[256,16]{0,1:T(8,128)(2,1)}, bf16[256,16]{0,1:T(8,128)(2,1)S(1)}, u32[]{:S(2)}) copy-start(bf16[256,16]{0,1:T(8,128)(2,1)S(1)} %multiply_convert_fusion.5) | copy-start | bytes 24580
  1466.6 375.7 %reduce-scatter.16.cloned.1.call-start = ((), (), s32[]{:S(2)}) async-start(), calls=%async_computation.19 | async-start | bytes 18874368
  1533.9 318.6 %reduce-scatter.18.cloned.1.call-start = ((), (), s32[]{:S(2)}) async-start(), calls=%async_computation.20 | async-start | bytes 18874368
  1602.5 285.7 %reduce-scatter.14.cloned.1.call-start = ((), (), s32[]{:S(2)}) async-start(), calls=%async_computation.17 | async-start | bytes 18874368 | tf_op jit(solution)/shard_map/reduce_scatter | solution.py:268
  1624.3 318.7 %all-reduce.11.cloned.1.call-start = ((), (), s32[]{:S(2)}) async-start(), calls=%async_computation.15 | async-start | bytes 2097152 | tf_op jit(solution)/shard_map/psum | solution.py:353
  1807.5 209.6 %reduce-scatter.12.cloned.1.call-start = ((), (), s32[]{:S(2)}) async-start(), calls=%async_computation.14 | async-start | bytes 9437184 | tf_op jit(solution)/shard_map/reduce_scatter | solution.py:332
  1828.0 410.5 %all-gather.15.cloned.1.call-start = ((), (), s32[]{:S(2)}) async-start(), calls=%async_computation.18 | async-start | bytes 15728640 | tf_op jit(solution)/shard_map/all_gather | solution.py:350
  1840.9 526.1 %all-reduce.13.cloned.1.call-start = ((), (), s32[]{:S(2)}) async-start(), calls=%async_computation.16 | async-start | bytes 262144 | tf_op jit(solution)/shard_map/psum | solution.py:355
  1862.8 156.9 %copy-start.9 = (f32[256,2048]{1,0:T(8,128)S(1)}, f32[256,2048]{1,0:T(8,128)}, u32[]{:S(2)}) copy-start(f32[256,2048]{1,0:T(8,128)} %copy-done.7) | copy-start | bytes 6291460
  1862.8 156.9 %copy-start.43 = (f32[2048]{0:T(1024)S(1)}, f32[2048]{0:T(1024)}, u32[]{:S(2)}) copy-start(f32[2048]{0:T(1024)} %param.27) | copy-start | bytes 24580
  1862.8 156.9 %copy-start.55 = (f32[256]{0:T(256)S(1)}, f32[256]{0:T(256)}, u32[]{:S(2)}) copy-start(f32[256]{0:T(256)} %copy-done.53) | copy-start | bytes 3076
  1862.8 156.9 %copy-start.63 = (f32[256]{0:T(256)S(1)}, f32[256]{0:T(256)}, u32[]{:S(2)}) copy-start(f32[256]{0:T(256)} %copy-done.62) | copy-start | bytes 3076
  (77 other events, 620.5 us)
Sparse Core Ops, SparseCore 0:
  103.0 118.8 reduce-scatter.9
  223.8 93.0 all-gather.6
  318.7 93.0 all-gather.8
  413.5 89.7 all-gather.10
  1466.7 52.3 all-gather.12
  1534.0 114.4 reduce-scatter.15
  1652.1 116.1 reduce-scatter.17
  1771.9 116.1 reduce-scatter.13
  1891.1 51.8 all-reduce.10
  1946.3 70.7 reduce-scatter.11
  2019.3 219.1 all-gather.14
  2244.4 122.5 all-reduce.12
